TPU v7x, 32 devices: a whole 2x2x4 slice. The times are simulated.
32 devices in a mesh: parts: 2 (over y), shot: 4 (over z), freq: 2 (over x), rep: 2 (over core).
Axes of the slice: x: 2, y: 2, z: 4, core: 2. Of those that a mesh axis runs over, the one named last changes fastest.
Arguments:
- recorded: bfloat16 [2, 4, 2048, 2048], P(None, ('parts', 'freq'), ('shot', 'rep')), parts along dimension 1, may hold values from -6 to 6
- receiver_x: float32 [4096], P('parts'), parts along dimension 0, may hold values from -12800 to 12800
- source_x: float32 [4096], P('parts'), parts along dimension 0, may hold values from -12800 to 12800
Outputs:
- predicted: bfloat16 [2, 4, 2048, 2048], P(None, ('parts', 'freq'), ('shot', 'rep')), parts along dimension 1
There are 2 independent parts, one for each index of `parts`. A program takes and returns all parts, laid end to end along the dimension named above; each array names one. Nothing has to cross between parts.
All inputs are finite; a program needn't handle non-finite values.
Results may differ from a plain program's by a relative error of at most 0.013.
Values may be sent and summed in bfloat16 or wider, within the bound.
A program may use at most 64 MiB of HBM per device.

v0:
```python
import math

import jax
import jax.numpy as jnp
from jax import lax
from jax.sharding import PartitionSpec as P

NSLOW = 1024


two_pi = 6.283185307179586
base_hertz = 40.0
step_hertz = 0.5
slow_max = 0.0005


def slowness_values(grid_count):
    counts = jnp.arange(grid_count, dtype=jnp.int32)
    return slow_max * ((2 * counts + 1 - grid_count).astype(jnp.float32) / grid_count)


def angle_columns(omegas, positions, slowness_grid):
    phases = (omegas[:, None] * slowness_grid[None, :])[:, None, :] * positions[None, :, None]
    return (jnp.cos(phases).astype(jnp.bfloat16), jnp.sin(phases).astype(jnp.bfloat16))


def angle_rows(omegas, positions, slowness_grid):
    phases = (omegas[:, None] * slowness_grid[None, :])[:, :, None] * positions[None, None, :]
    return (jnp.cos(phases).astype(jnp.bfloat16), jnp.sin(phases).astype(jnp.bfloat16))


def contract_product(form, left, right):
    return jnp.einsum(form, left, right, preferred_element_type=jnp.float32)


def receiver_forward(recorded, receiver_x, omegas, slowness_grid):
    data_real = recorded[0]
    data_imaginary = recorded[1]
    freq_count, shot_rows, rec_count = data_real.shape
    width_block = math.gcd(rec_count, 128)
    initial = jnp.zeros((freq_count, slowness_grid.shape[0], shot_rows), jnp.float32)

    def accumulate(loop_index, totals):
        first_row = loop_index * width_block
        positions = lax.dynamic_slice_in_dim(receiver_x, first_row, width_block, 0)
        cosine_lookup, sine_lookup = angle_columns(omegas, positions, slowness_grid)
        left_factor_real = lax.dynamic_slice_in_dim(data_real, first_row, width_block, 2)
        left_factor_imaginary = lax.dynamic_slice_in_dim(data_imaginary, first_row, width_block, 2)
        next_real = (
            totals[0]
            + contract_product("vqd,vdl->vlq", left_factor_real, cosine_lookup)
            + contract_product("vqd,vdl->vlq", left_factor_imaginary, sine_lookup)
        )
        next_imaginary = (
            totals[1]
            + contract_product("vqd,vdl->vlq", left_factor_imaginary, cosine_lookup)
            - contract_product("vqd,vdl->vlq", left_factor_real, sine_lookup)
        )
        return (next_real, next_imaginary)

    sum_real, sum_imaginary = lax.fori_loop(
        0, rec_count // width_block, accumulate, (initial, initial)
    )
    factor = 1.0 / math.sqrt(rec_count)
    return jnp.stack([sum_real * factor, sum_imaginary * factor], axis=1).astype(jnp.bfloat16)


def source_forward(gathered, source_x, omegas, slowness_grid):
    freq_count, parts_count, slice_rows, src_count = gathered.shape
    width_block = math.gcd(src_count, 128)
    initial = jnp.zeros((freq_count, slice_rows, slowness_grid.shape[0]), jnp.float32)

    def accumulate(loop_index, totals):
        first_row = loop_index * width_block
        positions = lax.dynamic_slice_in_dim(source_x, first_row, width_block, 0)
        cosine_lookup, sine_lookup = angle_columns(omegas, positions, slowness_grid)
        left_factor_real = lax.dynamic_slice_in_dim(gathered[:, 0], first_row, width_block, 2)
        left_factor_imaginary = lax.dynamic_slice_in_dim(gathered[:, 1], first_row, width_block, 2)
        next_real = (
            totals[0]
            + contract_product("fps,fsq->fpq", left_factor_real, cosine_lookup)
            + contract_product("fps,fsq->fpq", left_factor_imaginary, sine_lookup)
        )
        next_imaginary = (
            totals[1]
            + contract_product("fps,fsq->fpq", left_factor_imaginary, cosine_lookup)
            - contract_product("fps,fsq->fpq", left_factor_real, sine_lookup)
        )
        return (next_real, next_imaginary)

    sum_real, sum_imaginary = lax.fori_loop(
        0, src_count // width_block, accumulate, (initial, initial)
    )
    factor = 1.0 / math.sqrt(src_count)
    return ((sum_real * factor).astype(jnp.bfloat16), (sum_imaginary * factor).astype(jnp.bfloat16))


def make_fold(columns_real, columns_imaginary, pieces):
    next_real = contract_product("fpk,fkq->fpq", columns_real, pieces[0]) - contract_product(
        "fpk,fkq->fpq", columns_imaginary, pieces[1]
    )
    next_imaginary = contract_product("fpk,fkq->fpq", columns_real, pieces[1]) + contract_product(
        "fpk,fkq->fpq", columns_imaginary, pieces[0]
    )
    return (next_real, next_imaginary)


def source_inverse(multiple_real, multiple_imaginary, source_x, omegas, slowness_grid):
    freq_count, slice_rows, slow_count = multiple_real.shape
    src_count = source_x.shape[0]
    width_block = math.gcd(slow_count, 128)
    initial = jnp.zeros((freq_count, slice_rows, src_count), jnp.float32)

    def accumulate(loop_index, totals):
        first_row = loop_index * width_block
        block_slowness = lax.dynamic_slice_in_dim(slowness_grid, first_row, width_block, 0)
        cosine_lookup, sine_lookup = angle_rows(omegas, source_x, block_slowness)
        left_factor_real = lax.dynamic_slice_in_dim(multiple_real, first_row, width_block, 2)
        left_factor_imaginary = lax.dynamic_slice_in_dim(
            multiple_imaginary, first_row, width_block, 2
        )
        next_real = (
            totals[0]
            + contract_product("fpq,fqs->fps", left_factor_real, cosine_lookup)
            - contract_product("fpq,fqs->fps", left_factor_imaginary, sine_lookup)
        )
        next_imaginary = (
            totals[1]
            + contract_product("fpq,fqs->fps", left_factor_real, sine_lookup)
            + contract_product("fpq,fqs->fps", left_factor_imaginary, cosine_lookup)
        )
        return (next_real, next_imaginary)

    sum_real, sum_imaginary = lax.fori_loop(
        0, slow_count // width_block, accumulate, (initial, initial)
    )
    factor = 1.0 / math.sqrt(NSLOW)
    return jnp.stack([sum_real * factor, sum_imaginary * factor], axis=1).astype(jnp.bfloat16)


def receiver_inverse(returned, receiver_x, omegas, slowness_grid):
    freq_count, parts_count, slow_count, shot_rows = returned.shape
    rec_count = receiver_x.shape[0]
    width_block = math.gcd(slow_count, 128)
    initial = jnp.zeros((freq_count, shot_rows, rec_count), jnp.float32)

    def accumulate(loop_index, totals):
        first_row = loop_index * width_block
        block_slowness = lax.dynamic_slice_in_dim(slowness_grid, first_row, width_block, 0)
        cosine_lookup, sine_lookup = angle_rows(omegas, receiver_x, block_slowness)
        left_factor_real = lax.dynamic_slice_in_dim(returned[:, 0], first_row, width_block, 1)
        left_factor_imaginary = lax.dynamic_slice_in_dim(returned[:, 1], first_row, width_block, 1)
        next_real = (
            totals[0]
            + contract_product("kom,kox->kmx", left_factor_real, cosine_lookup)
            - contract_product("kom,kox->kmx", left_factor_imaginary, sine_lookup)
        )
        next_imaginary = (
            totals[1]
            + contract_product("kom,kox->kmx", left_factor_real, sine_lookup)
            + contract_product("kom,kox->kmx", left_factor_imaginary, cosine_lookup)
        )
        return (next_real, next_imaginary)

    sum_real, sum_imaginary = lax.fori_loop(
        0, slow_count // width_block, accumulate, (initial, initial)
    )
    factor = 1.0 / math.sqrt(NSLOW)
    return jnp.stack([sum_real * factor, sum_imaginary * factor], axis=0).astype(jnp.bfloat16)


def body(recorded, receiver_x, source_x):
    per_device = recorded.shape[1]
    first_freq = lax.axis_index("freq") * per_device
    indices = (first_freq + jnp.arange(per_device, dtype=jnp.int32)).astype(jnp.float32)
    omegas = two_pi * (base_hertz + step_hertz * indices)
    slowness_grid = slowness_values(NSLOW)
    spread = receiver_forward(recorded, receiver_x, omegas, slowness_grid)
    gathered = lax.all_to_all(spread, ("shot", "rep"), split_axis=2, concat_axis=3, tiled=True)
    plane_real, plane_imaginary = source_forward(gathered, source_x, omegas, slowness_grid)
    factor = 1.0 / math.sqrt(NSLOW)
    square_real, square_imaginary = make_fold(
        plane_real,
        plane_imaginary,
        (
            lax.all_gather(plane_real, ("shot", "rep"), axis=1, tiled=True),
            lax.all_gather(plane_imaginary, ("shot", "rep"), axis=1, tiled=True),
        ),
    )
    multiple_real = (square_real * factor).astype(jnp.bfloat16)
    multiple_imaginary = (square_imaginary * factor).astype(jnp.bfloat16)
    back = source_inverse(multiple_real, multiple_imaginary, source_x, omegas, slowness_grid)
    returned = lax.all_to_all(back, ("shot", "rep"), split_axis=3, concat_axis=2, tiled=True)
    return receiver_inverse(returned, receiver_x, omegas, slowness_grid)


def solution(mesh):
    return jax.shard_map(
        body,
        mesh=mesh,
        in_specs=(P(None, ("parts", "freq"), ("shot", "rep"), None), P("parts"), P("parts")),
        out_specs=P(None, ("parts", "freq"), ("shot", "rep"), None),
        check_vma=False,
    )
```

profile of v0, /device:TPU:0, one launch (start us, length us, event | category | flops | bytes accessed | tf_op | source)
XLA Modules:
  0.0 821.4 jit_solution(6965451396006254132)
XLA Ops:
  9.7 188.8 %while.64 = (s32[]{:T(128)}, f32[1,1024,256]{2,1,0:T(8,128)S(1)}, f32[1,1024,256]{2,1,0:T(8,128)S(1)}, f32[1]{0:T(128)}, f32[2048]{0:T(1024)S(1)}, /*index=5*/bf...) while((s32[]{:T(128)}, f32[1,1024,256]{2,1,0:T(8,128)S(1)}, ...), condition=%wide.region_1.0_spmd.clone, body=%wide.region_0.0_spmd.clone.sunk | while | flops 271060992 | bytes 8674514 | solution.py:61
  200.8 6.3 all-to-all-start
  207.7 26.0 %all-to-all-done = bf16[1,2,1024,256]{3,1,0,2:T(2,128)(2,1)S(1)} async-done(((bf16[1,2,1024,256]{3,1,0,2:T(2,128)(2,1)}), bf16[1,2,1024,256]{3,1,0,2:T(2,128)(2,1)S(1)}, u32[]{:S(2)}, u32[]{:S(2)}) %all-to-all-start) | async-done | bytes 1048608 | tf_op jit(solution)/shard_map/all_to_all | solution.py:179
  234.9 166.8 %while.65 = (s32[]{:T(128)}, f32[1,128,1024]{2,1,0:T(8,128)S(1)}, f32[1,128,1024]{2,1,0:T(8,128)S(1)}, bf16[1,2,128,2048]{3,2,1,0:T(8,128)(2,1)S(1)}, f32[1]{0:T...) while((s32[]{:T(128)}, f32[1,128,1024]{2,1,0:T(8,128)S(1)}, ...), condition=%wide.region_3.0_spmd.clone, body=%wide.region_2.0_spmd.clone.sunk | while | flops 136056832 | bytes 6446282 | solution.py:91
  403.4 27.4 %all-gather.5.cloned.1.call-done = bf16[1,1024,1024]{2,1,0:T(8,128)(2,1)} async-done(((bf16[1,128,1024]{2,1,0:T(8,128)(2,1)}), bf16[1,1024,1024]{2,1,0:T(8,128)(2,1)}) %all-gather.5.cloned.1.call-update) | async-done | bytes 2097168 | tf_op jit(solution)/shard_map/all_gather | solution.py:187
  434.3 26.7 %all-gather.3.cloned.1.call-done = bf16[1,1024,1024]{2,1,0:T(8,128)(2,1)} async-done(((bf16[1,128,1024]{2,1,0:T(8,128)(2,1)}), bf16[1,1024,1024]{2,1,0:T(8,128)(2,1)}) %all-gather.3.cloned.1.call-update) | async-done | bytes 2097168 | tf_op jit(solution)/shard_map/all_gather | solution.py:186
  464.3 132.1 %while.66 = (s32[]{:T(128)}, f32[1,128,2048]{2,1,0:T(8,128)S(1)}, f32[1,128,2048]{2,1,0:T(8,128)S(1)}, bf16[1,128,1024]{2,1,0:T(8,128)(2,1)S(1)}, f32[1]{0:T(128...) while((s32[]{:T(128)}, f32[1,128,2048]{2,1,0:T(8,128)S(1)}, ...), condition=%wide.region_5.0_spmd.clone, body=%wide.region_4.0_spmd.clone.sunk | while | flops 272105600 | bytes 8555718 | solution.py:134
  602.3 26.5 %all-to-all-done.1 = bf16[1,2,128,2048]{2,1,0,3:T(2,128)(2,1)S(1)} async-done(((bf16[1,2,128,2048]{2,1,0,3:T(2,128)(2,1)}), bf16[1,2,128,2048]{2,1,0,3:T(2,128)(2,1)S(1)}, u32[]{:S(2)}, u32[]{:S(2)}) %all-to-all-start.1) | async-done | bytes 1048608 | tf_op jit(solution)/shard_map/all_to_all | solution.py:193
  629.5 180.7 %while.67 = (s32[]{:T(128)}, f32[1,256,2048]{2,1,0:T(8,128)}, f32[1,256,2048]{2,1,0:T(8,128)}, bf16[1,2,1024,256]{3,2,1,0:T(8,128)(2,1)S(1)}, f32[1]{0:T(128)}, ...) while((s32[]{:T(128)}, f32[1,256,2048]{2,1,0:T(8,128)}, ...), condition=%wide.region_7.0_spmd.clone, body=%wide.region_6.0_spmd.clone.sunk | while | flops 542113920 | bytes 38046992 | solution.py:165
  635.0 5.9 fusion.255
  645.5 5.0 fusion.254
  657.2 6.2 fusion.255
  668.2 5.0 fusion.254
  679.9 6.2 fusion.255
  690.8 5.0 fusion.254
  702.5 6.2 fusion.255
  713.4 5.0 fusion.254
  725.1 6.2 fusion.255
  736.1 5.0 fusion.254
  747.8 6.2 fusion.255
  758.7 5.0 fusion.254
  770.4 6.2 fusion.255
  781.3 5.0 fusion.254
  793.0 6.2 fusion.255
  (377 shorter events, 607.7 us)
Async XLA Ops:
  6.5 3.2 copy-start.9
  200.8 32.9 %all-to-all-start = ((bf16[1,2,1024,256]{3,1,0,2:T(2,128)(2,1)}), bf16[1,2,1024,256]{3,1,0,2:T(2,128)(2,1)S(1)}, u32[]{:S(2)}, u32[]{:S(2)}) async-start(bf16[1,2,1024,256]{3,1,0,2:T(2,128)(2,1)} %copy.14), calls=%async_computation | async-start | bytes 2097152 | tf_op jit(solution)/shard_map/all_to_all | solution.py:179
  207.2 223.5 %all-gather.5.cloned.1.call-start = ((), (), s32[]{:S(2)}) async-start(), calls=%async_computation.3 | async-start | bytes 2359296 | tf_op jit(solution)/shard_map/all_gather | solution.py:187
  402.5 31.3 %copy-start.6 = (bf16[1,128,1024]{2,1,0:T(8,128)(2,1)S(1)}, bf16[1,128,1024]{2,1,0:T(8,128)(2,1)}, u32[]{:S(2)}) copy-start(bf16[1,128,1024]{2,1,0:T(8,128)(2,1)} %multiply_convert_fusion.6) | copy-start | bytes 786436
  402.5 58.4 %all-gather.3.cloned.1.call-start = ((), (), s32[]{:S(2)}) async-start(), calls=%async_computation.2 | async-start | bytes 2359296 | tf_op jit(solution)/shard_map/all_gather | solution.py:186
  430.7 3.1 copy-start.5
  434.2 29.6 %copy-start.7 = (bf16[1,128,1024]{2,1,0:T(8,128)(2,1)S(1)}, bf16[1,128,1024]{2,1,0:T(8,128)(2,1)}, u32[]{:S(2)}) copy-start(bf16[1,128,1024]{2,1,0:T(8,128)(2,1)} %multiply_convert_fusion.7) | copy-start | bytes 786436
  460.9 3.0 copy-start.4
  598.7 30.1 %all-to-all-start.1 = ((bf16[1,2,128,2048]{2,1,0,3:T(2,128)(2,1)}), bf16[1,2,128,2048]{2,1,0,3:T(2,128)(2,1)S(1)}, u32[]{:S(2)}, u32[]{:S(2)}) async-start(bf16[1,2,128,2048]{2,1,0,3:T(2,128)(2,1)} %copy.16), calls=%async_computation.1 | async-start | bytes 2097152 | tf_op jit(solution)/shard_map/all_to_all | solution.py:193
  640.8 4.7 copy-start
  650.5 1.3 copy-start.1
  663.5 4.7 copy-start
  673.1 1.3 copy-start.1
  686.1 4.7 copy-start
  695.8 1.3 copy-start.1
  708.7 4.7 copy-start
  718.4 1.3 copy-start.1
  731.4 4.7 copy-start
  741.0 1.3 copy-start.1
  754.0 4.7 copy-start
  763.7 1.3 copy-start.1
  776.6 4.7 copy-start
  799.3 4.7 copy-start
  810.3 2.2 copy-start.2
  (11 other events, 10.1 us)
Sparse Core Ops, SparseCore 0:
  402.6 28.0 all-gather.4
  432.3 28.5 all-gather.2
where the time goes:
time: 836 us; the launch traced here: 821 us
  matrix products  631 us (75%)
  waiting for transfers between devices  107 us (13%)
  local copies, waits for them, and re-layouts  49.9 us (6%)
  between operations  14 us (2%)
  starting transfers between devices  10.4 us (1%)
    dot_general x196, matrix products, contract_product(): return jnp.einsum(form, left, right, preferred_element_type=jnp.float32)  631 us
    all_gather x1, waiting for transfers between devices, body(): lax.all_gather(plane_imaginary, ('shot', 'rep'), axis=1, tiled=True)  27.4 us
    all_gather x1, waiting for transfers between devices, body(): lax.all_gather(plane_real, ('shot', 'rep'), axis=1, tiled=True)  26.7 us
    all_to_all x1, waiting for transfers between devices, body(): lax.all_to_all(back, ('shot', 'rep'), split_axis=3, concat_axis=2, tiled=...  26.5 us
    all_to_all x1, waiting for transfers between devices, body(): lax.all_to_all(spread, ('shot', 'rep'), split_axis=2, concat_axis=3, tile...  26 us
    while x48, local copies, waits for them, and re-layouts  16.8 us
  transfers between devices with their start and end apart: 4, of which 4 were waited for; matrix products, arithmetic and copies ran while one was open for 1% of the time, Pallas kernels for 0%

commit v1 on v0

v1 whole, which is shorter than its diff:
```python
import math

import jax
import jax.numpy as jnp
from jax import lax
from jax.sharding import PartitionSpec as P

NSLOW = 1024

two_pi = 6.283185307179586
base_hertz = 40.0
step_hertz = 0.5
slow_max = 0.0005
GROUP = ("shot", "rep")


def angle_table(omega, positions):
    half = NSLOW // 2
    fine = math.gcd(half, 16)
    unit = (omega * (slow_max / NSLOW)) * positions
    coarse = (jnp.arange(half // fine, dtype=jnp.int32) * (2 * fine)).astype(jnp.float32)[:, None] * unit
    small = (2 * jnp.arange(fine, dtype=jnp.int32) + 1).astype(jnp.float32)[:, None] * unit
    cos_a, sin_a = jnp.cos(coarse)[:, None], jnp.sin(coarse)[:, None]
    cos_b, sin_b = jnp.cos(small)[None], jnp.sin(small)[None]
    cosine = cos_a * cos_b - sin_a * sin_b
    sine = sin_a * cos_b + cos_a * sin_b
    return jnp.stack([cosine, sine]).astype(jnp.bfloat16).reshape(NSLOW, positions.shape[0])


def product(form, left, right):
    return jnp.einsum(form, left, right, preferred_element_type=jnp.float32)


def one_frequency(data, receiver_x, source_x, omega):
    shots = data.shape[1]
    src_count, rec_count = source_x.shape[0], receiver_x.shape[0]
    receiver = angle_table(omega, receiver_x)
    source = angle_table(omega, source_x)
    first = lax.axis_index(GROUP) * shots
    mine = angle_table(omega, lax.dynamic_slice_in_dim(source_x, first, shots, 0))
    spread = (product("csr,jr->csj", data, receiver) * math.sqrt(2.0 / rec_count)).astype(jnp.bfloat16)
    met = lax.all_to_all(spread, GROUP, split_axis=2, concat_axis=1, tiled=True)
    plane = (product("qs,csj->cqj", source, met) * math.sqrt(2.0 / src_count)).astype(jnp.bfloat16)
    planes = lax.all_gather(plane, GROUP, axis=2, tiled=True)
    sign = jnp.where(jnp.arange(NSLOW) < NSLOW // 2, 1.0, -1.0) * math.sqrt(2.0 / NSLOW)
    half_way = (product("qs,cqj->csj", mine, planes) * sign).astype(jnp.bfloat16)
    back_real = product("sm,mj->sj", half_way[0], planes[0]) - product("sm,mj->sj", half_way[1], planes[1])
    back_imaginary = product("sm,mj->sj", half_way[0], planes[1]) + product("sm,mj->sj", half_way[1], planes[0])
    back = (jnp.stack([back_real, back_imaginary]) * math.sqrt(1.0 / NSLOW)).astype(jnp.bfloat16)
    return (product("csj,jr->csr", back, receiver) * math.sqrt(2.0 / NSLOW)).astype(jnp.bfloat16)


def body(recorded, receiver_x, source_x):
    per_device = recorded.shape[1]
    first_freq = lax.axis_index("freq") * per_device
    outs = []
    for k in range(per_device):
        omega = two_pi * (base_hertz + step_hertz * (first_freq + k).astype(jnp.float32))
        outs.append(one_frequency(recorded[:, k], receiver_x, source_x, omega))
    return jnp.stack(outs, axis=1)


def solution(mesh):
    return jax.shard_map(
        body,
        mesh=mesh,
        in_specs=(P(None, ("parts", "freq"), ("shot", "rep"), None), P("parts"), P("parts")),
        out_specs=P(None, ("parts", "freq"), ("shot", "rep"), None),
        check_vma=False,
    )
```

time: 836 us -> 123 us (0.15); the launches traced: 821 us -> 122 us
  matrix products: 631 us -> 17 us
  local copies, waits for them, and re-layouts: 49.9 us -> 5.76 us
  waiting for transfers between devices: 107 us -> 66.1 us
    dot_general x196 -> x8, matrix products: 631 us -> 17 us  [product(): return jnp.einsum(form, left, right, preferred_element_type=jnp.float32)]
    all_to_all x2 -> x1, waiting for transfers between devices: 52.5 us -> 21.5 us  [one_frequency(): met = lax.all_to_all(spread, GROUP, split_axis=2, concat_axis=1, tiled=True)]
    slice x24 -> x0, local copies, waits for them, and re-layouts: 21.1 us -> none  [the longest x16 14.1 us: accumulate(): gathered[:, 0]]
    while x48 -> x0, local copies, waits for them, and re-layouts: 16.8 us -> none
    all_gather x2 -> x1, waiting for transfers between devices: 54 us -> 44.6 us  [one_frequency(): planes = lax.all_gather(plane, GROUP, axis=2, tiled=True)]
  transfers between devices with their start and end apart: 4 -> 2, of which waited for: 4 -> 2; matrix products, arithmetic and copies ran while one was open for 1% -> 5% of each run, Pallas kernels for 0% -> 0%
where the time goes in v1:
time: 123 us; the launch traced here: 122 us
  waiting for transfers between devices  66.1 us (54%)
  matrix products  17 us (14%)
  between operations  13.6 us (11%)
  other arithmetic  13.2 us (11%)
  starting transfers between devices  6.57 us (5%)
  local copies, waits for them, and re-layouts  5.76 us (5%)
    all_gather x1, waiting for transfers between devices, one_frequency(): planes = lax.all_gather(plane, GROUP, axis=2, tiled=True)  44.6 us
    all_to_all x1, waiting for transfers between devices, one_frequency(): met = lax.all_to_all(spread, GROUP, split_axis=2, concat_axis=1, tiled=True)  21.5 us
    dot_general x8, matrix products, product(): return jnp.einsum(form, left, right, preferred_element_type=jnp.float32)  17 us
    all_to_all x1, starting transfers between devices, one_frequency(): met = lax.all_to_all(spread, GROUP, split_axis=2, concat_axis=1, tiled=True)  6.35 us
    all_to_all x2, local copies, waits for them, and re-layouts, one_frequency(): met = lax.all_to_all(spread, GROUP, split_axis=2, concat_axis=1, tiled=True)  3.1 us
    cos x2, other arithmetic, angle_table(): cos_a, sin_a = (jnp.cos(coarse)[:, None], jnp.sin(coarse)[:, None])  2.82 us
    another operation x2, other arithmetic  2.68 us
  transfers between devices with their start and end apart: 2, of which 2 were waited for; matrix products, arithmetic and copies ran while one was open for 5% of the time, Pallas kernels for 0%

profile of v1, /device:TPU:0, one launch (start us, length us, event | category | flops | bytes accessed | tf_op | source)
XLA Modules:
  0.0 122.2 jit_solution(8296329761846689416)
XLA Ops:
  6.6 0.9 broadcast_multiply_fusion
  7.4 2.6 %multiply_cosine_fusion = (f32[32,2048]{1,0:T(8,128)S(1)}, f32[32,2048]{1,0:T(8,128)}, f32[32,2048]{1,0:T(8,128)S(1)}, f32[32,2048]{1,0:T(8,128)S(1)}) fusion(f32[2048]{0:T(1024)S(1)} %get-tuple-element.27, f32[32]{0:T(128)S(1)} %multiply_convert_fusion.3, f32[2048]{0:T(1024)S(1)} %get-tuple-element.28), kind=kLoop, calls=%fused_computation.37 | loop fusion | flops 131072 | bytes 1065088 | tf_op jit(solution)/shard_map/cos | solution.py:23
  10.0 1.7 %multiply_cosine_fusion.2 = (f32[16,2048]{1,0:T(8,128)S(1)}, f32[16,2048]{1,0:T(8,128)}, f32[16,2048]{1,0:T(8,128)S(1)}, f32[16,2048]{1,0:T(8,128)S(1)}) fusion(f32[2048]{0:T(1024)S(1)} %get-tuple-element.27, f32[16]{0:T(128)S(1)} %add_convert_fusion.2, f32[2048]{0:T(1024)S(1)} %get-tuple-element.28), kind=kLoop, calls=%fused_computation.41 | loop fusion | flops 65536 | bytes 540736 | tf_op jit(solution)/shard_map/cos | solution.py:24
  11.7 1.5 %multiply_subtract_fusion = (bf16[1,32,16,2048]{3,2,1,0:T(8,128)(2,1)S(1)}, bf16[1,32,16,2048]{3,2,1,0:T(8,128)(2,1)S(1)}) fusion(f32[16,2048]{1,0:T(8,128)S(1)} %get-tuple-element.25, f32[32,2048]{1,0:T(8,128)S(1)} %get-tuple-element.23, f32[16,2048]{1,0:T(8,128)S(1)} %get-tuple-element.26, f32[32,2048]{1,0:T(8,128)S(1)} %get-tuple-element.24), kind=kLoop, calls=%fused_computation.6 | loop fusion | flops 8388608 | bytes 4980736 | tf_op jit(solution)/shard_map/sub | solution.py:25
  13.2 0.4 maximum_convert_fusion
  13.6 2.4 %fusion.10 = bf16[2,256,1024]{1,2,0:T(8,128)(2,1)S(1)} fusion(bf16[1024,2048,1]{1,0,2:T(8,128)(2,1)S(1)} %bitcast.68, bf16[2,1,256,2048]{3,2,1,0:T(8,128)(2,1)S(1)} %copy-done), kind=kOutput, calls=%fused_computation.20 | convolution fusion | flops 2148532224 | bytes 7340032 | tf_op jit(solution)/shard_map/csr,jr->csj/dot_general | solution.py:31
  16.0 2.0 %copy.6 = bf16[2,256,1024]{1,0,2:T(2,128)(2,1)} copy(bf16[2,256,1024]{1,2,0:T(8,128)(2,1)S(1)} %fusion.10) | data formatting | bytes 2097152 | tf_op jit(solution)/shard_map/convert_element_type | solution.py:41
  18.1 6.4 %all-to-all-start = ((bf16[2,256,1024]{1,0,2:T(2,128)(2,1)}), bf16[2,256,1024]{1,0,2:T(2,128)(2,1)S(1)}, u32[]{:S(2)}, u32[]{:S(2)}) async-start(bf16[2,256,1024]{1,0,2:T(2,128)(2,1)} %copy.6), calls=%async_computation | async-start | bytes 2097152 | tf_op jit(solution)/shard_map/all_to_all | solution.py:42
  24.4 0.2 all-gather.2.cloned.1.call-start
  24.6 2.5 %subtract_convert_fusion = (bf16[1,32,16,2048]{3,2,1,0:T(8,128)(2,1)S(1)}, bf16[1,32,16,2048]{3,2,1,0:T(8,128)(2,1)S(1)}) fusion(f32[16,2048]{1,0:T(8,128)} %get-tuple-element.14, f32[32,2048]{1,0:T(8,128)} %get-tuple-element.12, f32[16,2048]{1,0:T(8,128)S(1)} %get-tuple-element.13, f32[32,2048]{1,0:T(8,128)S(1)} %get-tuple-element.11), kind=kLoop, calls=%fused_computation.4 | loop fusion | flops 8388608 | bytes 4980736 | tf_op jit(solution)/shard_map/convert.2
  27.1 2.3 %pad_maximum_fusion = bf16[2,32,16,2048]{3,2,1,0:T(8,128)(2,1)} fusion(bf16[1,32,16,2048]{3,2,1,0:T(8,128)(2,1)S(1)} %get-tuple-element.6, bf16[1,32,16,2048]{3,2,1,0:T(8,128)(2,1)S(1)} %get-tuple-element.5), kind=kLoop, calls=%fused_computation.1 | loop fusion | flops 2097152 | bytes 8388608 | tf_op jit(solution)/shard_map/stack | solution.py:27
  29.5 21.5 %all-to-all-done = bf16[2,256,1024]{1,0,2:T(2,128)(2,1)S(1)} async-done(((bf16[2,256,1024]{1,0,2:T(2,128)(2,1)}), bf16[2,256,1024]{1,0,2:T(2,128)(2,1)S(1)}, u32[]{:S(2)}, u32[]{:S(2)}) %all-to-all-start) | async-done | bytes 1048608 | tf_op jit(solution)/shard_map/all_to_all | solution.py:42
  51.0 1.6 %copy.10 = bf16[2,256,8,128]{1,2,3,0:T(8,128)(2,1)} copy(bf16[2,256,8,128]{1,0,3,2:T(2,128)(2,1)S(1)} %bitcast.71) | data formatting | bytes 2097152 | tf_op jit(solution)/shard_map/all_to_all | solution.py:42
  52.5 1.6 %all_to_all.16 = bf16[2,2048,128]{1,2,0:T(8,128)(2,1)S(1)} reshape(bf16[2,8,256,128]{2,1,3,0:T(8,128)(2,1)} %bitcast.72) | data formatting | bytes 2097152 | tf_op jit(solution)/shard_map/all_to_all | solution.py:42
  54.1 4.3 %fusion.19 = bf16[2,1024,128]{1,2,0:T(8,128)(2,1)} fusion(bf16[2,2048,128]{1,2,0:T(8,128)(2,1)S(1)} %all_to_all.16, bf16[1024,2048,1]{1,0,2:T(8,128)(2,1)} %bitcast.70), kind=kOutput, calls=%fused_computation.28 | convolution fusion | flops 1074266112 | bytes 5767168 | tf_op jit(solution)/shard_map/qs,csj->cqj/dot_general | solution.py:31
  58.4 0.8 dynamic-slice_multiply_fusion
  59.8 44.6 %all-gather.2.cloned.1.call-done = bf16[2,1024,1024]{1,2,0:T(8,128)(2,1)} async-done(((bf16[2,1024,128]{1,2,0:T(8,128)(2,1)}), bf16[2,1024,1024]{1,2,0:T(8,128)(2,1)}) %all-gather.2.cloned.1.call-update) | async-done | bytes 4194320 | tf_op jit(solution)/shard_map/all_gather | solution.py:44
  104.3 3.6 %fusion.13 = bf16[2,256,1024]{1,2,0:T(8,128)(2,1)S(1)} fusion(bf16[2,1024,1024]{1,2,0:T(8,128)(2,1)} %all-gather.2.cloned.1.call-done, bf16[1024,256,1]{1,0,2:T(8,128)(2,1)S(1)} %bitcast.73, f32[1024]{0:T(1024)S(1)} %select_multiply_fusion), kind=kOutput, calls=%fused_computation.21 | convolution fusion | flops 1074790400 | bytes 5771264 | tf_op jit(solution)/shard_map/qs,cqj->csj/dot_general | solution.py:31
  107.9 0.8 fusion.5
  108.7 0.8 fusion.4
  109.5 0.8 fusion.15
  110.3 0.8 fusion.17
  111.1 0.6 copy-done.2
  111.7 3.7 %fusion = bf16[2,1,256,2048]{3,2,1,0:T(8,128)(2,1)} fusion(bf16[1024,2048,1]{1,0,2:T(8,128)(2,1)S(1)} %bitcast.69, f32[1,256,1024]{2,1,0:T(8,128)S(1)} %fusion.17, f32[1,256,1024]{2,1,0:T(8,128)S(1)} %fusion.15), kind=kOutput, calls=%fused_computation.7 | convolution fusion | flops 2151153664 | bytes 8388608 | tf_op jit(solution)/shard_map/csj,jr->csr/dot_general | solution.py:31
  (15 shorter events, 0.6 us)
Async XLA Ops:
  6.5 7.1 %copy-start = (bf16[2,1,256,2048]{3,2,1,0:T(8,128)(2,1)S(1)}, bf16[2,1,256,2048]{3,2,1,0:T(8,128)(2,1)}, u32[]{:S(2)}) copy-start(bf16[2,1,256,2048]{3,2,1,0:T(8,128)(2,1)} %param.3) | copy-start | bytes 6291460
  13.6 2.4 %copy-start.1 = (bf16[2,32,16,2048]{3,2,1,0:T(8,128)(2,1)}, bf16[2,32,16,2048]{3,2,1,0:T(8,128)(2,1)S(1)}, u32[]{:S(2)}) copy-start(bf16[2,32,16,2048]{3,2,1,0:T(8,128)(2,1)S(1)} %maximum_convert_fusion) | copy-start | bytes 12582916
  18.1 32.9 %all-to-all-start = ((bf16[2,256,1024]{1,0,2:T(2,128)(2,1)}), bf16[2,256,1024]{1,0,2:T(2,128)(2,1)S(1)}, u32[]{:S(2)}, u32[]{:S(2)}) async-start(bf16[2,256,1024]{1,0,2:T(2,128)(2,1)} %copy.6), calls=%async_computation | async-start | bytes 2097152 | tf_op jit(solution)/shard_map/all_to_all | solution.py:42
  24.4 79.9 %all-gather.2.cloned.1.call-start = ((), (), s32[]{:S(2)}) async-start(), calls=%async_computation.1 | async-start | bytes 4718592 | tf_op jit(solution)/shard_map/all_gather | solution.py:44
  104.3 3.6 %copy-start.3 = (bf16[2,1024,1024]{1,2,0:T(8,128)(2,1)S(1)}, bf16[2,1024,1024]{1,2,0:T(8,128)(2,1)}, u32[]{:S(2)}) copy-start(bf16[2,1024,1024]{1,2,0:T(8,128)(2,1)} %all-gather.2.cloned.1.call-done) | copy-start | bytes 12582916
  109.5 2.2 %copy-start.2 = (bf16[2,32,16,2048]{3,2,1,0:T(8,128)(2,1)S(1)}, bf16[2,32,16,2048]{3,2,1,0:T(8,128)(2,1)}, u32[]{:S(2)}) copy-start(bf16[2,32,16,2048]{3,2,1,0:T(8,128)(2,1)} %copy-done.1) | copy-start | bytes 12582916
Sparse Core Ops, SparseCore 0:
  58.5 45.7 all-gather.1

commit v2 on v1

--- a/solution.py
+++ b/solution.py
@@ -1,8 +1,11 @@
+import functools
 import math
 
 import jax
 import jax.numpy as jnp
 from jax import lax
+from jax.experimental import pallas as pl
+from jax.experimental.pallas import tpu as pltpu
 from jax.sharding import PartitionSpec as P
 
 NSLOW = 1024
@@ -50,19 +53,286 @@
     return (product("csj,jr->csr", back, receiver) * math.sqrt(2.0 / NSLOW)).astype(jnp.bfloat16)
 
 
-def body(recorded, receiver_x, source_x):
+FINE = 16
+HALF = NSLOW // 2
+COARSE = HALF // FINE
+MESH = pl.DeviceIdType.MESH
+
+
+def angle_factors(omega, positions):
+    unit = (omega * (slow_max / NSLOW)) * positions
+    steps = jnp.concatenate(
+        [jnp.arange(COARSE, dtype=jnp.int32) * (2 * FINE), 2 * jnp.arange(FINE, dtype=jnp.int32) + 1]
+    )
+    phases = steps.astype(jnp.float32)[:, None] * unit[None, :]
+    return jnp.stack([jnp.cos(phases), jnp.sin(phases)])
+
+
+def fill_table(factors, table):
+    count = table.shape[1]
+    tile = math.gcd(count, 512)
+    for first in range(0, count, tile):
+        lanes = slice(first, first + tile)
+        cos_b = factors[0, COARSE : COARSE + FINE, lanes]
+        sin_b = factors[1, COARSE : COARSE + FINE, lanes]
+
+        def step(a, carry):
+            cos_a = factors[0, pl.ds(a, 1), lanes]
+            sin_a = factors[1, pl.ds(a, 1), lanes]
+            row = pl.multiple_of(a * FINE, FINE)
+            table[pl.ds(row, FINE), lanes] = (cos_a * cos_b - sin_a * sin_b).astype(jnp.bfloat16)
+            table[pl.ds(HALF + row, FINE), lanes] = (sin_a * cos_b + cos_a * sin_b).astype(jnp.bfloat16)
+            return carry
+
+        lax.fori_loop(0, COARSE, step, 0, unroll=4)
+
+
+def dot(left, right):
+    return jnp.dot(left, right, preferred_element_type=jnp.float32)
+
+
+def whole_kernel(
+    chips, data, receiver_f, source_f, out,
+    receiver, source, mine, outgoing, met, planes, half_way, back,
+    spread_send, spread_recv, plane_send, plane_recv,
+):
+    cores = 2
+    group = chips * cores
+    width = NSLOW // group
+    shots = data.shape[0] // 2
+    z, c = lax.axis_index("shot"), lax.axis_index("rep")
+    me = z * cores + c
+
+    def place(d):
+        return {"shot": d // cores, "rep": d % cores}
+
+    barrier = pltpu.get_barrier_semaphore()
+    for d in range(group):
+        @pl.when(d != me)
+        def _():
+            pl.semaphore_signal(barrier, inc=1, device_id=place(d), device_id_type=MESH)
+
+    fill_table(receiver_f, receiver)
+    pl.semaphore_wait(barrier, group - 1)
+
+    def spread_copy(d):
+        return pltpu.make_async_remote_copy(
+            src_ref=outgoing.at[d], dst_ref=met.at[pl.ds(pl.multiple_of(me * shots, shots), shots)],
+            send_sem=spread_send.at[d], recv_sem=spread_recv.at[me], device_id=place(d), device_id_type=MESH,
+        )
+
+    scale = math.sqrt(2.0 / data.shape[1])
+    order = sorted(range(1, chips), key=lambda k: abs(2 * k - chips)) + [0]
+    for offset in order:
+        target = lax.rem(z + offset, chips)
+        rows = receiver[pl.ds(pl.multiple_of(target * (cores * width), cores * width), cores * width), :]
+        part = lax.dot_general(data[...], rows, (((1,), (1,)), ((), ())), preferred_element_type=jnp.float32)
+        part = (part * scale).astype(jnp.bfloat16)
+        for e in range(cores):
+            d = target * cores + e
+            real = part[:shots, e * width : (e + 1) * width]
+            imaginary = part[shots:, e * width : (e + 1) * width]
+            outgoing[d, :, :width] = real
+            outgoing[d, :, width:] = imaginary
+            if offset == 0:
+                @pl.when(d == me)
+                def _():
+                    own = pl.ds(pl.multiple_of(me * shots, shots), shots)
+                    met[own, :width] = real
+                    met[own, width:] = imaginary
+
+                @pl.when(d != me)
+                def _():
+                    spread_copy(d).start()
+            else:
+                spread_copy(d).start()
+
+    fill_table(source_f, source)
+    local = source[:, pl.ds(pl.multiple_of(me * shots, shots), shots)]
+    mine[...] = local.T
+
+    for d in range(group):
+        @pl.when(d != me)
+        def _():
+            pltpu.make_async_remote_copy(
+                src_ref=outgoing.at[d], dst_ref=met.at[pl.ds(d * shots, shots)],
+                send_sem=spread_send.at[d], recv_sem=spread_recv.at[d], device_id=place(d), device_id_type=MESH,
+            ).wait_recv()
+
+    scale = math.sqrt(2.0 / source.shape[1])
+    tile = 256
+
+    def plane_rows(i, carry):
+        rows = pl.ds(pl.multiple_of(i * tile, tile), tile)
+        planes[me, rows, :] = (dot(source[rows, :], met[...]) * scale).astype(jnp.bfloat16)
+        return carry
+
+    lax.fori_loop(0, NSLOW // tile, plane_rows, 0)
+
+    def plane_copy(way, d):
+        to = [{"shot": z + 1, "rep": c}, {"shot": z - 1, "rep": c}, {"shot": z, "rep": 1 - c}][way]
+        return pltpu.make_async_remote_copy(
+            src_ref=planes.at[d], dst_ref=planes.at[d], send_sem=plane_send.at[way, d], recv_sem=plane_recv.at[d],
+            device_id=to, device_id_type=MESH,
+        )
+
+    def half_slice(d):
+        sign = (1 - 2 * (d // (group // 2))).astype(jnp.float32)
+        part = (dot(mine[...], planes[d]) * math.sqrt(2.0 / NSLOW) * sign).astype(jnp.bfloat16)
+        lanes = pl.ds(pl.multiple_of(d * width, width), width)
+        half_way[:shots, lanes] = part[:, :width]
+        half_way[shots:, lanes] = part[:, width:]
+
+    more_up, more_down = z < chips - 1, z > 0
+
+    @pl.when(more_up)
+    def _():
+        plane_copy(0, me).start()
+
+    @pl.when(more_down)
+    def _():
+        plane_copy(1, me).start()
+
+    plane_copy(2, me).start()
+    half_slice(me)
+    for k in range(1, chips):
+        for way, sign in ((0, -1), (1, 1)):
+            origin = z + sign * k
+
+            @pl.when((origin >= 0) & (origin < chips))
+            def _():
+                d = origin * cores + c
+                plane_copy(2, d).wait_recv()
+
+                @pl.when((more_up, more_down)[way])
+                def _():
+                    plane_copy(way, d).start()
+
+                plane_copy(2, d).start()
+                half_slice(d)
+
+        for sign in ((-1, 1) if k > 1 else (1,)):
+            origin = z + sign * (k - 1)
+
+            @pl.when((origin >= 0) & (origin < chips))
+            def _():
+                d = origin * cores + 1 - c
+                plane_copy(2, d).wait_recv()
+                half_slice(d)
+
+    for sign in (-1, 1):
+        origin = z + sign * (chips - 1)
+
+        @pl.when((origin >= 0) & (origin < chips))
+        def _():
+            d = origin * cores + 1 - c
+            plane_copy(2, d).wait_recv()
+            half_slice(d)
+
+    scale_back = math.sqrt(1.0 / NSLOW)
+
+    def back_slice(d, carry):
+        both = dot(half_way[...], planes[d])
+        lanes = pl.ds(pl.multiple_of(d * width, width), width)
+        back[:shots, lanes] = ((both[:shots, :width] - both[shots:, width:]) * scale_back).astype(jnp.bfloat16)
+        back[shots:, lanes] = ((both[:shots, width:] + both[shots:, :width]) * scale_back).astype(jnp.bfloat16)
+        return carry
+
+    lax.fori_loop(0, group, back_slice, 0)
+    scale_out = math.sqrt(2.0 / NSLOW)
+    wide = math.gcd(out.shape[1], 512)
+
+    def out_columns(i, carry):
+        lanes = pl.ds(pl.multiple_of(i * wide, wide), wide)
+        out[:, lanes] = (dot(back[...], receiver[:, lanes]) * scale_out).astype(jnp.bfloat16)
+        return carry
+
+    lax.fori_loop(0, out.shape[1] // wide, out_columns, 0)
+
+    for d in range(group):
+        @pl.when(d != me)
+        def _():
+            spread_copy(d).wait_send()
+    plane_copy(2, me).wait_send()
+
+    @pl.when(more_up)
+    def _():
+        plane_copy(0, me).wait_send()
+
+    @pl.when(more_down)
+    def _():
+        plane_copy(1, me).wait_send()
+
+    for k in range(1, chips):
+        for way, sign in ((0, -1), (1, 1)):
+            origin = z + sign * k
+
+            @pl.when((origin >= 0) & (origin < chips))
+            def _():
+                d = origin * cores + c
+
+                @pl.when((more_up, more_down)[way])
+                def _():
+                    plane_copy(way, d).wait_send()
+
+                plane_copy(2, d).wait_send()
+
+
+def one_frequency_fused(chips, data, receiver_x, source_x, omega):
+    shots, rec_count = data.shape[1:]
+    src_count = source_x.shape[0]
+    group = 2 * chips
+    width = NSLOW // group
+    vmem = pl.BlockSpec(memory_space=pltpu.VMEM)
+    half = jnp.bfloat16
+    result = pl.pallas_call(
+        functools.partial(whole_kernel, chips),
+        out_shape=jax.ShapeDtypeStruct((2 * shots, rec_count), half),
+        in_specs=[vmem] * 3,
+        out_specs=vmem,
+        scratch_shapes=[
+            pltpu.VMEM((NSLOW, rec_count), half),
+            pltpu.VMEM((NSLOW, src_count), half),
+            pltpu.VMEM((shots, NSLOW), half),
+            pltpu.VMEM((group, shots, 2 * width), half),
+            pltpu.VMEM((src_count, 2 * width), half),
+            pltpu.VMEM((group, NSLOW, 2 * width), half),
+            pltpu.VMEM((2 * shots, NSLOW), half),
+            pltpu.VMEM((2 * shots, NSLOW), half),
+            pltpu.SemaphoreType.DMA((group,)),
+            pltpu.SemaphoreType.DMA((group,)),
+            pltpu.SemaphoreType.DMA((3, group)),
+            pltpu.SemaphoreType.DMA((group,)),
+        ],
+        compiler_params=pltpu.CompilerParams(
+            collective_id=0, has_side_effects=True, vmem_limit_bytes=60 * 1024 * 1024
+        ),
+        name="plane_wave_multiples",
+    )(data.reshape(2 * shots, rec_count), angle_factors(omega, receiver_x), angle_factors(omega, source_x))
+    return result.reshape(2, shots, rec_count)
+
+
+def fits(mesh_shape, shots):
+    group = mesh_shape["shot"] * mesh_shape["rep"]
+    return mesh_shape["rep"] == 2 and NSLOW % (128 * group) == 0 and shots % 128 == 0
+
+
+def body(chips, fused, recorded, receiver_x, source_x):
     per_device = recorded.shape[1]
     first_freq = lax.axis_index("freq") * per_device
     outs = []
     for k in range(per_device):
         omega = two_pi * (base_hertz + step_hertz * (first_freq + k).astype(jnp.float32))
-        outs.append(one_frequency(recorded[:, k], receiver_x, source_x, omega))
+        if fused(recorded.shape[2]):
+            outs.append(one_frequency_fused(chips, recorded[:, k], receiver_x, source_x, omega))
+        else:
+            outs.append(one_frequency(recorded[:, k], receiver_x, source_x, omega))
     return jnp.stack(outs, axis=1)
 
 
 def solution(mesh):
     return jax.shard_map(
-        body,
+        functools.partial(body, mesh.shape["shot"], functools.partial(fits, mesh.shape)),
         mesh=mesh,
         in_specs=(P(None, ("parts", "freq"), ("shot", "rep"), None), P("parts"), P("parts")),
         out_specs=P(None, ("parts", "freq"), ("shot", "rep"), None),

time: 123 us -> 87.7 us (0.71)
  Pallas kernels: 0 us -> 78.8 us
  waiting for transfers between devices: 66.1 us -> 0 us
  matrix products: 17 us -> 0 us
  between operations: 13.6 us -> 0.02 us
  other arithmetic: 13.2 us -> 5.49 us
  starting transfers between devices: 6.57 us -> 0 us
  local copies, waits for them, and re-layouts: 5.76 us -> 3.16 us
    pallas_call x0 -> x1, Pallas kernels: none -> 78.8 us  [one_frequency_fused(): pl.pallas_call(functools.partial(whole_kernel, chips), out_shape=jax.Shap...]
    all_gather x1 -> x0, waiting for transfers between devices: 44.6 us -> none  [one_frequency(): planes = lax.all_gather(plane, GROUP, axis=2, tiled=True)]
    all_to_all x1 -> x0, waiting for transfers between devices: 21.5 us -> none  [one_frequency(): met = lax.all_to_all(spread, GROUP, split_axis=2, concat_axis=1, tiled=True)]
    dot_general x8 -> x0, matrix products: 17 us -> none  [product(): return jnp.einsum(form, left, right, preferred_element_type=jnp.float32)]
    all_to_all x1 -> x0, starting transfers between devices: 6.35 us -> none  [one_frequency(): met = lax.all_to_all(spread, GROUP, split_axis=2, concat_axis=1, tiled=True)]
    another operation x4 -> x2, other arithmetic: 5.07 us -> 1.9 us  [angle_factors(): return jnp.stack([jnp.cos(phases), jnp.sin(phases)])]
    all_to_all x2 -> x0, local copies, waits for them, and re-layouts: 3.1 us -> none  [one_frequency(): met = lax.all_to_all(spread, GROUP, split_axis=2, concat_axis=1, tiled=True)]
    unnamed x8 -> x1, local copies, waits for them, and re-layouts: 0.61 us -> 3.16 us
  transfers between devices with their start and end apart: 2 -> 0, of which waited for: 2 -> 0; matrix products, arithmetic and copies ran while one was open for 5% -> 0% of each run, Pallas kernels for 0% -> 0%
where the time goes in v2:
time: 87.7 us; the launch traced here: 87.4 us
  Pallas kernels  78.8 us (90%)
  other arithmetic  5.49 us (6%)
  local copies, waits for them, and re-layouts  3.16 us (4%)
    pallas_call x1, Pallas kernels, one_frequency_fused(): pl.pallas_call(functools.partial(whole_kernel, chips), out_shape=jax.Shap...  78.8 us
    unnamed x1, local copies, waits for them, and re-layouts  3.16 us
    cos x1, other arithmetic, angle_factors(): return jnp.stack([jnp.cos(phases), jnp.sin(phases)])  2.79 us
    another operation x2, other arithmetic, angle_factors(): return jnp.stack([jnp.cos(phases), jnp.sin(phases)])  1.9 us

profile of v2, /device:TPU:0, one launch (start us, length us, event | category | flops | bytes accessed | tf_op | source)
XLA Modules:
  0.0 87.4 jit_solution(9562096473543847788)
XLA Ops:
  0.0 0.1 add_convert_fusion
  0.1 0.7 broadcast_multiply_fusion
  0.8 2.8 %multiply_cosine_fusion = (f32[1,48,2048]{2,1,0:T(8,128)S(1)}, f32[1,48,2048]{2,1,0:T(8,128)S(1)}, f32[1,48,2048]{2,1,0:T(8,128)S(1)}, f32[1,48,2048]{2,1,0:T(8,128)S(1)}) fusion(f32[2048]{0:T(1024)S(1)} %get-tuple-element.11, f32[48]{0:T(128)S(1)} %add_convert_fusion, f32[2048]{0:T(1024)S(1)} %get-tuple-element.12), kind=kLoop, calls=%fused_computation.3 | loop fusion | flops 196608 | bytes 1589440 | tf_op jit(solution)/shard_map/cos | solution.py:68
  3.6 1.0 %pad_maximum_fusion.1.source_f = f32[2,48,2048]{2,1,0:T(8,128)} fusion(f32[1,48,2048]{2,1,0:T(8,128)S(1)} %get-tuple-element.6, f32[1,48,2048]{2,1,0:T(8,128)S(1)} %get-tuple-element.5), kind=kLoop, calls=%fused_computation.1 | loop fusion | flops 196608 | bytes 1572864 | tf_op jit(solution)/shard_map/stack | solution.py:68
  4.6 0.9 %pad_maximum_fusion.receiver_f = f32[2,48,2048]{2,1,0:T(8,128)} fusion(f32[1,48,2048]{2,1,0:T(8,128)S(1)} %get-tuple-element.9, f32[1,48,2048]{2,1,0:T(8,128)S(1)} %get-tuple-element.10), kind=kLoop, calls=%fused_computation | loop fusion | flops 196608 | bytes 1572864 | tf_op jit(solution)/shard_map/stack | solution.py:68
  5.5 78.8 %plane_wave_multiples.1 = bf16[512,2048]{1,0:T(8,128)(2,1)} custom-call(bf16[512,2048]{1,0:T(8,128)(2,1)} %bitcast.5, f32[2,48,2048]{2,1,0:T(8,128)} %pad_maximum_fusion.receiver_f, f32[2,48,2048]{2,1,0:T(8,128)} %pad_maximum_fusion.1.source_f), custom_call_target="tpu_custom_call" | custom-call | tf_op jit(solution)/shard_map/plane_wave_multiples/pallas_call | solution.py:288
  84.3 3.2 %copy.6 = bf16[2,1,256,2048]{3,2,1,0:T(8,128)(2,1)} copy(bf16[2,1,256,2048]{3,2,1,0:T(8,128)(2,1)} %bitcast.4) | data formatting | bytes 4194304
  (2 shorter events, 0.0 us)

commit v3 on v2

v3 whole, which is shorter than its diff:
```python
import functools
import math

import jax
import jax.numpy as jnp
from jax import lax
from jax.experimental import pallas as pl
from jax.experimental.pallas import tpu as pltpu
from jax.sharding import PartitionSpec as P

NSLOW = 1024

two_pi = 6.283185307179586
base_hertz = 40.0
step_hertz = 0.5
slow_max = 0.0005
GROUP = ("shot", "rep")


def angle_table(omega, positions):
    half = NSLOW // 2
    fine = math.gcd(half, 16)
    unit = (omega * (slow_max / NSLOW)) * positions
    coarse = (jnp.arange(half // fine, dtype=jnp.int32) * (2 * fine)).astype(jnp.float32)[:, None] * unit
    small = (2 * jnp.arange(fine, dtype=jnp.int32) + 1).astype(jnp.float32)[:, None] * unit
    cos_a, sin_a = jnp.cos(coarse)[:, None], jnp.sin(coarse)[:, None]
    cos_b, sin_b = jnp.cos(small)[None], jnp.sin(small)[None]
    cosine = cos_a * cos_b - sin_a * sin_b
    sine = sin_a * cos_b + cos_a * sin_b
    return jnp.stack([cosine, sine]).astype(jnp.bfloat16).reshape(NSLOW, positions.shape[0])


def product(form, left, right):
    return jnp.einsum(form, left, right, preferred_element_type=jnp.float32)


def one_frequency(data, receiver_x, source_x, omega):
    shots = data.shape[1]
    src_count, rec_count = source_x.shape[0], receiver_x.shape[0]
    receiver = angle_table(omega, receiver_x)
    source = angle_table(omega, source_x)
    first = lax.axis_index(GROUP) * shots
    mine = angle_table(omega, lax.dynamic_slice_in_dim(source_x, first, shots, 0))
    spread = (product("csr,jr->csj", data, receiver) * math.sqrt(2.0 / rec_count)).astype(jnp.bfloat16)
    met = lax.all_to_all(spread, GROUP, split_axis=2, concat_axis=1, tiled=True)
    plane = (product("qs,csj->cqj", source, met) * math.sqrt(2.0 / src_count)).astype(jnp.bfloat16)
    planes = lax.all_gather(plane, GROUP, axis=2, tiled=True)
    sign = jnp.where(jnp.arange(NSLOW) < NSLOW // 2, 1.0, -1.0) * math.sqrt(2.0 / NSLOW)
    half_way = (product("qs,cqj->csj", mine, planes) * sign).astype(jnp.bfloat16)
    back_real = product("sm,mj->sj", half_way[0], planes[0]) - product("sm,mj->sj", half_way[1], planes[1])
    back_imaginary = product("sm,mj->sj", half_way[0], planes[1]) + product("sm,mj->sj", half_way[1], planes[0])
    back = (jnp.stack([back_real, back_imaginary]) * math.sqrt(1.0 / NSLOW)).astype(jnp.bfloat16)
    return (product("csj,jr->csr", back, receiver) * math.sqrt(2.0 / NSLOW)).astype(jnp.bfloat16)


FINE = 16
HALF = NSLOW // 2
COARSE = HALF // FINE
MESH = pl.DeviceIdType.MESH


def fill_factors(omega, positions, factors):
    count = positions.shape[1]
    tile = math.gcd(count, 256)
    sines = [(-1.0) ** n / math.factorial(2 * n + 1) for n in range(7)]
    cosines = [(-1.0) ** n / math.factorial(2 * n) for n in range(8)]
    turn_high = 6.28125
    turn_low = two_pi - turn_high

    def step(i, carry):
        lanes = pl.ds(pl.multiple_of(i * tile, tile), tile)
        unit = positions[:, lanes] * (omega * (slow_max / NSLOW))
        row = lax.broadcasted_iota(jnp.int32, (COARSE + FINE, tile), 0)
        steps = jnp.where(row < COARSE, row * (2 * FINE), 2 * (row - COARSE) + 1).astype(jnp.float32)
        phase = steps * unit
        turns = jnp.floor(phase * (1.0 / two_pi) + 0.5)
        half = 0.5 * ((phase - turns * turn_high) - turns * turn_low)
        square = half * half
        sine, cosine = sines[-1], cosines[-1]
        for term in reversed(sines[:-1]):
            sine = sine * square + term
        for term in reversed(cosines[:-1]):
            cosine = cosine * square + term
        sine = sine * half
        factors[0, :, lanes] = 1.0 - 2.0 * sine * sine
        factors[1, :, lanes] = 2.0 * sine * cosine
        return carry

    lax.fori_loop(0, count // tile, step, 0)


def fill_table(factors, table):
    count = table.shape[1]
    tile = math.gcd(count, 512)
    for first in range(0, count, tile):
        lanes = slice(first, first + tile)
        cos_b = factors[0, COARSE : COARSE + FINE, lanes]
        sin_b = factors[1, COARSE : COARSE + FINE, lanes]

        def step(a, carry):
            cos_a = factors[0, pl.ds(a, 1), lanes]
            sin_a = factors[1, pl.ds(a, 1), lanes]
            row = pl.multiple_of(a * FINE, FINE)
            table[pl.ds(row, FINE), lanes] = (cos_a * cos_b - sin_a * sin_b).astype(jnp.bfloat16)
            table[pl.ds(HALF + row, FINE), lanes] = (sin_a * cos_b + cos_a * sin_b).astype(jnp.bfloat16)
            return carry

        lax.fori_loop(0, COARSE, step, 0, unroll=4)


def dot(left, right):
    return jnp.dot(left, right, preferred_element_type=jnp.float32)


def whole_kernel(
    chips, first_hertz, data, receiver_x, source_x, out,
    receiver, source, receiver_f, source_f, mine, outgoing, met, planes, half_way, back,
    spread_send, spread_recv, plane_send, plane_recv,
):
    cores = 2
    group = chips * cores
    width = NSLOW // group
    shots = data.shape[0] // 2
    z, c = lax.axis_index("shot"), lax.axis_index("rep")
    me = z * cores + c

    def place(d):
        return {"shot": d // cores, "rep": d % cores}

    barrier = pltpu.get_barrier_semaphore()
    for d in range(group):
        @pl.when(d != me)
        def _():
            pl.semaphore_signal(barrier, inc=1, device_id=place(d), device_id_type=MESH)

    hertz = first_hertz(lax.axis_index("freq")).astype(jnp.float32)
    omega = two_pi * (base_hertz + step_hertz * hertz)
    fill_factors(omega, receiver_x, receiver_f)
    fill_table(receiver_f, receiver)
    pl.semaphore_wait(barrier, group - 1)

    def spread_copy(h, d):
        return pltpu.make_async_remote_copy(
            src_ref=outgoing.at[h, d], dst_ref=met.at[h, pl.ds(pl.multiple_of(me * shots, shots), shots)],
            send_sem=spread_send.at[h, d], recv_sem=spread_recv.at[h, me],
            device_id=place(d), device_id_type=MESH,
        )

    scale = math.sqrt(2.0 / data.shape[1])
    order = sorted(range(1, chips), key=lambda k: abs(2 * k - chips)) + [0]
    for h in range(2):
        for offset in order:
            target = lax.rem(z + offset, chips)
            rows = receiver[pl.ds(pl.multiple_of(target * (cores * width), cores * width), cores * width), :]
            part = lax.dot_general(
                data[h * shots : (h + 1) * shots, :], rows, (((1,), (1,)), ((), ())),
                preferred_element_type=jnp.float32,
            )
            part = (part * scale).astype(jnp.bfloat16)
            for e in range(cores):
                d = target * cores + e
                piece = part[:, e * width : (e + 1) * width]
                if offset == 0:
                    @pl.when(d == me)
                    def _():
                        met[h, pl.ds(pl.multiple_of(me * shots, shots), shots), :] = piece

                    @pl.when(d != me)
                    def _():
                        outgoing[h, d] = piece
                        spread_copy(h, d).start()
                else:
                    outgoing[h, d] = piece
                    spread_copy(h, d).start()

    fill_factors(omega, source_x, source_f)
    fill_table(source_f, source)
    local = source[:, pl.ds(pl.multiple_of(me * shots, shots), shots)]
    mine[...] = local.T

    def plane_copy(way, h, d):
        to = [{"shot": z + 1, "rep": c}, {"shot": z - 1, "rep": c}, {"shot": z, "rep": 1 - c}][way]
        piece = planes.at[d, :, h * width : (h + 1) * width]
        return pltpu.make_async_remote_copy(
            src_ref=piece, dst_ref=piece, send_sem=plane_send.at[way, h, d], recv_sem=plane_recv.at[h, d],
            device_id=to, device_id_type=MESH,
        )

    scale = math.sqrt(2.0 / source.shape[1])
    tile = 256
    more_up, more_down = z < chips - 1, z > 0
    for h in range(2):
        for d in range(group):
            @pl.when(d != me)
            def _():
                pltpu.make_async_remote_copy(
                    src_ref=outgoing.at[h, d], dst_ref=met.at[h, pl.ds(d * shots, shots)],
                    send_sem=spread_send.at[h, d], recv_sem=spread_recv.at[h, d],
                    device_id=place(d), device_id_type=MESH,
                ).wait_recv()

        def plane_rows(i, carry):
            rows = pl.ds(pl.multiple_of(i * tile, tile), tile)
            piece = (dot(source[rows, :], met[h]) * scale).astype(jnp.bfloat16)
            planes[me, rows, h * width : (h + 1) * width] = piece
            return carry

        lax.fori_loop(0, NSLOW // tile, plane_rows, 0)

        @pl.when(more_up)
        def _():
            plane_copy(0, h, me).start()

        @pl.when(more_down)
        def _():
            plane_copy(1, h, me).start()

        plane_copy(2, h, me).start()

    def half_slice(d):
        sign = (1 - 2 * (d // (group // 2))).astype(jnp.float32)
        part = (dot(mine[...], planes[d]) * math.sqrt(2.0 / NSLOW) * sign).astype(jnp.bfloat16)
        lanes = pl.ds(pl.multiple_of(d * width, width), width)
        half_way[:shots, lanes] = part[:, :width]
        half_way[shots:, lanes] = part[:, width:]

    half_slice(me)
    for k in range(1, chips):
        for h in range(2):
            for way, sign in ((0, -1), (1, 1)):
                origin = z + sign * k

                @pl.when((origin >= 0) & (origin < chips))
                def _():
                    d = origin * cores + c
                    plane_copy(2, h, d).wait_recv()

                    @pl.when((more_up, more_down)[way])
                    def _():
                        plane_copy(way, h, d).start()

                    plane_copy(2, h, d).start()
                    if h == 1:
                        half_slice(d)

        for sign in ((-1, 1) if k > 1 else (1,)):
            origin = z + sign * (k - 1)

            @pl.when((origin >= 0) & (origin < chips))
            def _():
                d = origin * cores + 1 - c
                plane_copy(2, 0, d).wait_recv()
                plane_copy(2, 1, d).wait_recv()
                half_slice(d)

    for sign in (-1, 1):
        origin = z + sign * (chips - 1)

        @pl.when((origin >= 0) & (origin < chips))
        def _():
            d = origin * cores + 1 - c
            plane_copy(2, 0, d).wait_recv()
            plane_copy(2, 1, d).wait_recv()
            half_slice(d)

    scale_back = math.sqrt(1.0 / NSLOW)

    def back_slice(d, carry):
        both = dot(half_way[...], planes[d])
        lanes = pl.ds(pl.multiple_of(d * width, width), width)
        back[:shots, lanes] = ((both[:shots, :width] - both[shots:, width:]) * scale_back).astype(jnp.bfloat16)
        back[shots:, lanes] = ((both[:shots, width:] + both[shots:, :width]) * scale_back).astype(jnp.bfloat16)
        return carry

    lax.fori_loop(0, group, back_slice, 0)
    scale_out = math.sqrt(2.0 / NSLOW)
    wide = math.gcd(out.shape[1], 512)

    def out_columns(i, carry):
        lanes = pl.ds(pl.multiple_of(i * wide, wide), wide)
        out[:, lanes] = (dot(back[...], receiver[:, lanes]) * scale_out).astype(jnp.bfloat16)
        return carry

    lax.fori_loop(0, out.shape[1] // wide, out_columns, 0)

    for h in range(2):
        for d in range(group):
            @pl.when(d != me)
            def _():
                spread_copy(h, d).wait_send()
        plane_copy(2, h, me).wait_send()

        @pl.when(more_up)
        def _():
            plane_copy(0, h, me).wait_send()

        @pl.when(more_down)
        def _():
            plane_copy(1, h, me).wait_send()

        for k in range(1, chips):
            for way, sign in ((0, -1), (1, 1)):
                origin = z + sign * k

                @pl.when((origin >= 0) & (origin < chips))
                def _():
                    d = origin * cores + c

                    @pl.when((more_up, more_down)[way])
                    def _():
                        plane_copy(way, h, d).wait_send()

                    plane_copy(2, h, d).wait_send()


def one_frequency_fused(chips, first_hertz, data, receiver_x, source_x):
    shots, rec_count = data.shape[1:]
    src_count = source_x.shape[0]
    group = 2 * chips
    width = NSLOW // group
    vmem = pl.BlockSpec(memory_space=pltpu.VMEM)
    half = jnp.bfloat16
    result = pl.pallas_call(
        functools.partial(whole_kernel, chips, first_hertz),
        out_shape=jax.ShapeDtypeStruct((2 * shots, rec_count), half),
        in_specs=[vmem] * 3,
        out_specs=vmem,
        scratch_shapes=[
            pltpu.VMEM((NSLOW, rec_count), half),
            pltpu.VMEM((NSLOW, src_count), half),
            pltpu.VMEM((2, COARSE + FINE, rec_count), jnp.float32),
            pltpu.VMEM((2, COARSE + FINE, src_count), jnp.float32),
            pltpu.VMEM((shots, NSLOW), half),
            pltpu.VMEM((2, group, shots, width), half),
            pltpu.VMEM((2, src_count, width), half),
            pltpu.VMEM((group, NSLOW, 2 * width), half),
            pltpu.VMEM((2 * shots, NSLOW), half),
            pltpu.VMEM((2 * shots, NSLOW), half),
            pltpu.SemaphoreType.DMA((2, group)),
            pltpu.SemaphoreType.DMA((2, group)),
            pltpu.SemaphoreType.DMA((3, 2, group)),
            pltpu.SemaphoreType.DMA((2, group)),
        ],
        compiler_params=pltpu.CompilerParams(
            collective_id=0, has_side_effects=True, vmem_limit_bytes=60 * 1024 * 1024
        ),
        name="plane_wave_multiples",
    )(data.reshape(2 * shots, rec_count), receiver_x.reshape(1, rec_count), source_x.reshape(1, src_count))
    return result.reshape(2, shots, rec_count)


def fits(mesh_shape, shots):
    group = mesh_shape["shot"] * mesh_shape["rep"]
    return mesh_shape["rep"] == 2 and NSLOW % (128 * group) == 0 and shots % 128 == 0


def body(chips, fused, recorded, receiver_x, source_x):
    per_device = recorded.shape[1]
    first_freq = lax.axis_index("freq") * per_device
    outs = []
    for k in range(per_device):
        omega = two_pi * (base_hertz + step_hertz * (first_freq + k).astype(jnp.float32))
        if fused(recorded.shape[2]):
            first_hertz = functools.partial(lambda k, f: f * per_device + k, k)
            outs.append(one_frequency_fused(chips, first_hertz, recorded[:, k], receiver_x, source_x))
        else:
            outs.append(one_frequency(recorded[:, k], receiver_x, source_x, omega))
    return jnp.stack(outs, axis=1)


def solution(mesh):
    return jax.shard_map(
        functools.partial(body, mesh.shape["shot"], functools.partial(fits, mesh.shape)),
        mesh=mesh,
        in_specs=(P(None, ("parts", "freq"), ("shot", "rep"), None), P("parts"), P("parts")),
        out_specs=P(None, ("parts", "freq"), ("shot", "rep"), None),
        check_vma=False,
    )
```

time: 87.7 us -> 76.3 us (0.87)
  Pallas kernels: 78.8 us -> 73 us
  other arithmetic: 5.49 us -> 0 us
    pallas_call x1, Pallas kernels: 78.8 us -> 73 us  [one_frequency_fused(): pl.pallas_call(functools.partial(whole_kernel, chips, first_hertz), out_s...]
    cos x1 -> x0, other arithmetic: 2.79 us -> none  [angle_factors(): return jnp.stack([jnp.cos(phases), jnp.sin(phases)])]
    another operation x2 -> x0, other arithmetic: 1.9 us -> none  [angle_factors(): return jnp.stack([jnp.cos(phases), jnp.sin(phases)])]
where the time goes in v3:
time: 76.3 us; the launch traced here: 76.2 us
  Pallas kernels  73 us (96%)
  local copies, waits for them, and re-layouts  3.16 us (4%)
    pallas_call x1, Pallas kernels, one_frequency_fused(): pl.pallas_call(functools.partial(whole_kernel, chips, first_hertz), out_s...  73 us
    unnamed x1, local copies, waits for them, and re-layouts  3.16 us

profile of v3, /device:TPU:0, one launch (start us, length us, event | category | flops | bytes accessed | tf_op | source)
XLA Modules:
  0.0 76.2 jit_solution(3558414513325048119)
XLA Ops:
  0.0 73.0 %plane_wave_multiples.1 = bf16[512,2048]{1,0:T(8,128)(2,1)} custom-call(bf16[512,2048]{1,0:T(8,128)(2,1)} %bitcast.7, f32[1,2048]{1,0:T(1,128)} %bitcast.8, f32[1,2048]{1,0:T(1,128)} %bitcast.9), custom_call_target="tpu_custom_call" | custom-call | tf_op jit(solution)/shard_map/plane_wave_multiples/pallas_call | solution.py:323
  73.0 3.2 %copy.6 = bf16[2,1,256,2048]{3,2,1,0:T(8,128)(2,1)} copy(bf16[2,1,256,2048]{3,2,1,0:T(8,128)(2,1)} %bitcast.6) | data formatting | bytes 4194304

commit v4 on v3

--- a/solution.py
+++ b/solution.py
@@ -113,9 +113,9 @@
 
 
 def whole_kernel(
-    chips, first_hertz, data, receiver_x, source_x, out,
-    receiver, source, receiver_f, source_f, mine, outgoing, met, planes, half_way, back,
-    spread_send, spread_recv, plane_send, plane_recv,
+    chips, first_hertz, data, receiver_x, source_x, back, kept,
+    receiver, source, receiver_f, source_f, mine, outgoing, met, planes, half_way,
+    spread_send, spread_recv, plane_send, plane_recv, kept_sem,
 ):
     cores = 2
     group = chips * cores
@@ -173,6 +173,9 @@
                     outgoing[h, d] = piece
                     spread_copy(h, d).start()
 
+    keep = pltpu.make_async_copy(receiver, kept, kept_sem)
+    keep.start()
+
     fill_factors(omega, source_x, source_f)
     fill_table(source_f, source)
     local = source[:, pl.ds(pl.multiple_of(me * shots, shots), shots)]
@@ -273,16 +276,7 @@
         return carry
 
     lax.fori_loop(0, group, back_slice, 0)
-    scale_out = math.sqrt(2.0 / NSLOW)
-    wide = math.gcd(out.shape[1], 512)
-
-    def out_columns(i, carry):
-        lanes = pl.ds(pl.multiple_of(i * wide, wide), wide)
-        out[:, lanes] = (dot(back[...], receiver[:, lanes]) * scale_out).astype(jnp.bfloat16)
-        return carry
-
-    lax.fori_loop(0, out.shape[1] // wide, out_columns, 0)
-
+    keep.wait()
     for h in range(2):
         for d in range(group):
             @pl.when(d != me)
@@ -320,11 +314,14 @@
     width = NSLOW // group
     vmem = pl.BlockSpec(memory_space=pltpu.VMEM)
     half = jnp.bfloat16
-    result = pl.pallas_call(
+    back, receiver = pl.pallas_call(
         functools.partial(whole_kernel, chips, first_hertz),
-        out_shape=jax.ShapeDtypeStruct((2 * shots, rec_count), half),
+        out_shape=(
+            jax.ShapeDtypeStruct((2 * shots, NSLOW), half),
+            jax.ShapeDtypeStruct((NSLOW, rec_count), half),
+        ),
         in_specs=[vmem] * 3,
-        out_specs=vmem,
+        out_specs=(vmem, pl.BlockSpec(memory_space=pl.ANY)),
         scratch_shapes=[
             pltpu.VMEM((NSLOW, rec_count), half),
             pltpu.VMEM((NSLOW, src_count), half),
@@ -335,17 +332,18 @@
             pltpu.VMEM((2, src_count, width), half),
             pltpu.VMEM((group, NSLOW, 2 * width), half),
             pltpu.VMEM((2 * shots, NSLOW), half),
-            pltpu.VMEM((2 * shots, NSLOW), half),
             pltpu.SemaphoreType.DMA((2, group)),
             pltpu.SemaphoreType.DMA((2, group)),
             pltpu.SemaphoreType.DMA((3, 2, group)),
             pltpu.SemaphoreType.DMA((2, group)),
+            pltpu.SemaphoreType.DMA,
         ],
         compiler_params=pltpu.CompilerParams(
             collective_id=0, has_side_effects=True, vmem_limit_bytes=60 * 1024 * 1024
         ),
         name="plane_wave_multiples",
     )(data.reshape(2 * shots, rec_count), receiver_x.reshape(1, rec_count), source_x.reshape(1, src_count))
+    result = (dot(back, receiver) * math.sqrt(2.0 / NSLOW)).astype(half)
     return result.reshape(2, shots, rec_count)
 
 

time: 76.3 us -> 76.1 us (level)
  matrix products: 0 us -> 6.17 us
  Pallas kernels: 73 us -> 69.8 us
  local copies, waits for them, and re-layouts: 3.16 us -> 0 us
    dot_general x0 -> x1, matrix products: none -> 6.17 us  [dot(): return jnp.dot(left, right, preferred_element_type=jnp.float32)]
    pallas_call x1, Pallas kernels: 73 us -> 69.8 us  [one_frequency_fused(): pl.pallas_call(functools.partial(whole_kernel, chips, first_hertz), out_s...]
    unnamed x1 -> x0, local copies, waits for them, and re-layouts: 3.16 us -> none
where the time goes in v4:
time: 76.1 us; the launch traced here: 76 us
  Pallas kernels  69.8 us (92%)
  matrix products  6.17 us (8%)
    pallas_call x1, Pallas kernels, one_frequency_fused(): pl.pallas_call(functools.partial(whole_kernel, chips, first_hertz), out_s...  69.8 us
    dot_general x1, matrix products, dot(): return jnp.dot(left, right, preferred_element_type=jnp.float32)  6.17 us

profile of v4, /device:TPU:0, one launch (start us, length us, event | category | flops | bytes accessed | tf_op | source)
XLA Modules:
  0.0 76.0 jit_solution(14691916894093547634)
XLA Ops:
  0.0 69.8 %plane_wave_multiples.1 = (bf16[512,1024]{1,0:T(8,128)(2,1)}, bf16[1024,2048]{1,0:T(8,128)(2,1)}) custom-call(bf16[512,2048]{1,0:T(8,128)(2,1)} %bitcast.8, f32[1,2048]{1,0:T(1,128)} %bitcast.9, f32[1,2048]{1,0:T(1,128)} %bitcast.10), custom_call_target="tpu_custom_call" | custom-call | tf_op jit(solution)/shard_map/plane_wave_multiples/pallas_call | solution.py:317
  69.8 6.2 %multiply_convert_fusion = bf16[512,2048]{1,0:T(8,128)(2,1)} fusion(bf16[512,1024]{1,0:T(8,128)(2,1)} %get-tuple-element.7, bf16[1024,2048]{1,0:T(8,128)(2,1)} %get-tuple-element.8), kind=kOutput, calls=%fused_computation | convolution fusion | flops 2149580800 | bytes 7340032 | tf_op jit(solution)/shard_map/dot_general | solution.py:112
